TPU v7x, 16 devices: a whole 2x2x2 slice. The times are simulated.
16 devices in a mesh: vp: 2 (over z), dp: 8 (over y, x, core).
Axes of the slice: x: 2, y: 2, z: 2, core: 2. Of those that a mesh axis runs over, the one named last changes fastest.
Arguments:
- student_x: bfloat16 [1280, 1536], P('dp')
- teacher_x: bfloat16 [256, 1536], P('dp')
- w_in: bfloat16 [1536, 2048], replicated
- b_in: bfloat16 [2048], replicated
- w_mid: bfloat16 [2048, 2048], replicated
- b_mid: bfloat16 [2048], replicated
- w_out: bfloat16 [2048, 384], replicated
- b_out: bfloat16 [384], replicated
- protos: bfloat16 [384, 131072], P(None, 'vp')
- ema_w_in: bfloat16 [1536, 2048], replicated
- ema_b_in: bfloat16 [2048], replicated
- ema_w_mid: bfloat16 [2048, 2048], replicated
- ema_b_mid: bfloat16 [2048], replicated
- ema_w_out: bfloat16 [2048, 384], replicated
- ema_b_out: bfloat16 [384], replicated
- ema_protos: bfloat16 [384, 131072], P(None, 'vp')
Outputs:
- output 1: float32 [], replicated
- output 2: float32 [1536, 2048], replicated
- output 3: float32 [2048], replicated
- output 4: float32 [2048, 2048], replicated
- output 5: float32 [2048], replicated
- output 6: float32 [2048, 384], replicated
- output 7: float32 [384], replicated
- output 8: float32 [384, 131072], P(None, 'vp')
All inputs are finite; a program needn't handle non-finite values.
Results may differ from a plain program's by a relative error of at most 0.00516174.
Values sent between devices are 32-bit elements.
A program may use at most 1 GiB of HBM per device.

v0:
```python
import jax
import jax.numpy as jnp
from jax import lax
from jax.sharding import PartitionSpec as P

ALL_CROPS = 10
GLOBAL_CROPS = 2
SINK_ITERS = 3
TEMP_STUDENT = 0.1
TEMP_TEACHER = 0.04


def gelu_slope(pre):
    cdf = 0.5 * (1.0 + lax.erf(pre * 0.7071067811865476))
    return cdf + pre * jnp.exp(-0.5 * pre * pre) * 0.3989422804014327


def mlp_forward(feats, w_in, b_in, w_mid, b_mid, w_out, b_out):
    pre_one = jnp.dot(feats, w_in, preferred_element_type=jnp.float32) + b_in.astype(jnp.float32)
    hid_one = jax.nn.gelu(pre_one, approximate=False).astype(jnp.bfloat16)
    pre_two = jnp.dot(hid_one, w_mid, preferred_element_type=jnp.float32) + b_mid.astype(jnp.float32)
    hid_two = jax.nn.gelu(pre_two, approximate=False).astype(jnp.bfloat16)
    proj = jnp.dot(hid_two, w_out, preferred_element_type=jnp.float32) + b_out.astype(jnp.float32)
    inv_norm = lax.rsqrt(jnp.sum(proj * proj, axis=-1, keepdims=True))
    unit = proj * inv_norm
    return unit.astype(jnp.bfloat16), (pre_one, hid_one, pre_two, hid_two, unit, inv_norm)


def mlp_backward(g_emb, feats, saved, w_mid, w_out):
    pre_one, hid_one, pre_two, hid_two, unit, inv_norm = saved
    g_proj = (g_emb - unit * jnp.sum(unit * g_emb, axis=-1, keepdims=True)) * inv_norm
    g_proj_lo = g_proj.astype(jnp.bfloat16)
    g_w_out = jnp.einsum('nh,nb->hb', hid_two, g_proj_lo, preferred_element_type=jnp.float32)
    g_hid_two = jnp.einsum('nb,hb->nh', g_proj_lo, w_out, preferred_element_type=jnp.float32)
    g_pre_two = g_hid_two.astype(jnp.bfloat16).astype(jnp.float32) * gelu_slope(pre_two)
    g_pre_two_lo = g_pre_two.astype(jnp.bfloat16)
    g_w_mid = jnp.einsum('ng,nh->gh', hid_one, g_pre_two_lo, preferred_element_type=jnp.float32)
    g_hid_one = jnp.einsum('nh,gh->ng', g_pre_two_lo, w_mid, preferred_element_type=jnp.float32)
    g_pre_one = g_hid_one.astype(jnp.bfloat16).astype(jnp.float32) * gelu_slope(pre_one)
    g_w_in = jnp.einsum('nf,nh->fh', feats, g_pre_one.astype(jnp.bfloat16), preferred_element_type=jnp.float32)
    return (g_w_in, jnp.sum(g_pre_one, axis=0), g_w_mid, jnp.sum(g_pre_two, axis=0), g_w_out, jnp.sum(g_proj, axis=0))


def col_normalize(protos):
    proto_f = protos.astype(jnp.float32)
    inv_col = lax.rsqrt(jnp.sum(proto_f * proto_f, axis=0, keepdims=True))
    unit = proto_f * inv_col
    return unit.astype(jnp.bfloat16), unit, inv_col


def col_normalize_backward(g_unit, unit, inv_col):
    return (g_unit - unit * jnp.sum(unit * g_unit, axis=0, keepdims=True)) * inv_col


def pair_targets(q_three):
    pad_rows = ALL_CROPS - GLOBAL_CROPS
    return jnp.sum(q_three, axis=1, keepdims=True) - jnp.pad(q_three, ((0, 0), (0, pad_rows), (0, 0)))


def crop_counts():
    crop_idx = jnp.arange(ALL_CROPS)
    return (GLOBAL_CROPS - (crop_idx < GLOBAL_CROPS).astype(jnp.int32)).astype(jnp.float32)


def solution(mesh):
    vp_size = mesh.shape['vp']
    dp_size = mesh.shape['dp']

    def local_step(student_x, teacher_x, w_in, b_in, w_mid, b_mid, w_out, b_out, protos,
                   ema_w_in, ema_b_in, ema_w_mid, ema_b_mid, ema_w_out, ema_b_out, ema_protos):
        n_img = student_x.shape[0] // ALL_CROPS
        local_proto = protos.shape[1]
        n_proto = local_proto * vp_size
        n_rows = GLOBAL_CROPS * n_img * dp_size
        t_emb, _ = mlp_forward(teacher_x, ema_w_in, ema_b_in, ema_w_mid, ema_b_mid, ema_w_out, ema_b_out)
        t_unit = col_normalize(ema_protos)[0]
        q_mat = jnp.exp(jnp.dot(t_emb, t_unit, preferred_element_type=jnp.float32) / TEMP_TEACHER)
        q_mat = q_mat / lax.psum(jnp.sum(q_mat), ('vp', 'dp'))
        for _ in range(SINK_ITERS):
            proto_sum = lax.psum(jnp.sum(q_mat, axis=0, keepdims=True), 'dp')
            q_mat = q_mat / (proto_sum * n_proto)
            crop_sum = lax.psum(jnp.sum(q_mat, axis=1, keepdims=True), 'vp')
            q_mat = q_mat / (crop_sum * n_rows)
        q_three = (q_mat * n_rows).reshape(n_img, GLOBAL_CROPS, local_proto)

        s_emb, saved = mlp_forward(student_x, w_in, b_in, w_mid, b_mid, w_out, b_out)
        s_unit, unit_f, inv_col = col_normalize(protos)
        logits = jnp.dot(s_emb, s_unit, preferred_element_type=jnp.float32) / TEMP_STUDENT
        logits = logits.reshape(n_img, ALL_CROPS, local_proto)
        row_max = lax.pmax(jnp.max(logits, axis=-1, keepdims=True), 'vp')
        shifted = logits - row_max
        exp_s = jnp.exp(shifted)
        row_sum = lax.psum(jnp.sum(exp_s, axis=-1, keepdims=True), 'vp')
        scale = 1.0 / (n_img * dp_size * GLOBAL_CROPS * (ALL_CROPS - 1))
        targets = pair_targets(q_three)
        loss = lax.psum(jnp.sum(targets * (jnp.log(row_sum) - shifted)), ('vp', 'dp')) * scale
        g_logits = (crop_counts()[:, None] * (exp_s / row_sum) - targets) * (scale / TEMP_STUDENT)
        g_logits = g_logits.reshape(n_img * ALL_CROPS, local_proto).astype(jnp.bfloat16)
        g_emb = jnp.einsum('rk,bk->rb', g_logits, s_unit, preferred_element_type=jnp.float32)
        g_unit = lax.psum(jnp.einsum('rb,rk->bk', s_emb, g_logits, preferred_element_type=jnp.float32), 'dp')
        head_grads = lax.psum(mlp_backward(g_emb, student_x, saved, w_mid, w_out), ('vp', 'dp'))
        g_protos = col_normalize_backward(g_unit, unit_f, inv_col)
        return (loss,) + tuple(head_grads) + (g_protos,)

    by_rows = P('dp', None)
    by_cols = P(None, 'vp')
    replicated = P()
    head_specs = (replicated,) * 6
    in_specs = (by_rows, by_rows) + head_specs + (by_cols,) + head_specs + (by_cols,)
    out_specs = (replicated,) * 7 + (by_cols,)
    return jax.shard_map(local_step, mesh=mesh, in_specs=in_specs, out_specs=out_specs, check_vma=False)
```

profile of v0, /device:TPU:0, one launch (start us, length us, event | category | flops | bytes accessed | tf_op | source)
XLA Modules:
  0.0 2024.9 jit_solution(1659070618255024926)
XLA Ops:
  7.2 0.0 all-reduce.10.cloned.1.call-start
  7.2 0.8 convert_element_type.91
  8.0 0.7 convert_element_type.93
  8.7 0.7 convert_element_type.95
  9.4 4.7 fusion.65
  14.1 5.6 multiply_reduce_fusion.3
  19.7 16.1 fusion.3
  35.9 24.0 %fusion.154 = (f32[]{:T(128)}, f32[32,65536]{1,0:T(8,128)}) fusion(bf16[384,65536]{1,0:T(8,128)(2,1)} %param.31, f32[65536]{0:T(1024)S(1)} %rsqrt.33, f32[32,384]{1,0:T(8,128)S(1)} %get-tuple-element.38, f32[32]{0:T(128)S(1)} %rsqrt.32), kind=kOutput, calls=%fused_computation.224 | convolution fusion | flops 1690329088 | bytes 59031684 | tf_op jit(solution)/shard_map/dot_general | solution.py:77
  59.9 34.7 %psum.112 = f32[]{:T(128)} all-reduce(f32[]{:T(128)} %get-tuple-element.39), channel_id=1, replica_groups=mesh['vp'=2,'dp'=8] {'vp','dp'}, use_global_device_ids=true, to_apply=%region_3.0 | all-reduce | flops 1 | bytes 8 | tf_op jit(solution)/shard_map/psum | solution.py:78
  94.6 5.7 divide_reduce_fusion
  100.3 0.0 all-reduce.10.cloned.1.call-update
  100.3 0.6 all-reduce.12.cloned.1.call-start
  101.0 16.2 fusion.8
  117.2 4.1 convolution_add_fusion
  121.3 10.8 fusion.36
  132.1 0.8 copy-done.5
  132.9 0.6 multiply_reduce_fusion.2
  134.3 13.2 all-reduce.10.cloned.1.call-done
  147.5 1.1 broadcast_multiply_fusion.2
  148.7 4.2 divide_reduce_fusion.1
  152.9 4.9 psum.114
  157.8 5.8 fusion.23
  163.6 0.2 all-reduce.14.cloned.1.call-start
  163.8 30.3 %fusion.155 = (f32[160]{0:T(256)S(1)}, f32[160,65536]{1,0:T(8,128)}) fusion(bf16[384,65536]{1,0:T(8,128)(2,1)} %param.24, f32[65536]{0:T(1024)S(1)} %rsqrt.35, f32[160,384]{1,0:T(8,128)S(1)} %get-tuple-element.44, f32[160]{0:T(256)S(1)} %rsqrt.34), kind=kOutput, calls=%fused_computation.225 | convolution fusion | flops 8149655552 | bytes 92783872 | tf_op jit(solution)/shard_map/dot_general | solution.py:88
  194.1 0.1 broadcast_in_dim.43
  194.2 5.0 pmax.7
  199.2 0.1 sub.53
  199.3 10.0 all-reduce.12.cloned.1.call-done
  209.3 1.2 broadcast_multiply_fusion.1
  210.4 4.3 fusion.24
  214.8 4.9 psum.116
  219.7 6.5 fusion.25
  226.2 0.0 all-reduce.18.cloned.1.call-start
  226.3 16.8 exponential_reduce_fusion
  243.0 46.5 %reshape.68 = f32[16,10,65536]{2,1,0:T(8,128)} reshape(f32[160,65536]{1,0:T(8,128)} %get-tuple-element.46) | data formatting | bytes 83886080 | tf_op jit(solution)/shard_map/reshape | solution.py:89
  289.5 0.1 broadcast_in_dim.44
  289.6 0.0 all-reduce.14.cloned.1.call-done
  289.6 1.2 broadcast_multiply_fusion
  290.8 4.6 fusion.26
  295.4 5.2 all-reduce.3
  300.7 6.7 fusion.22
  307.4 9.3 reshape.67
  316.7 13.3 reduce_sum.180
  330.0 38.0 %multiply_convert_fusion = (bf16[16,10,65536]{2,1,0:T(8,128)(2,1)}, f32[]{:T(128)}) fusion(f32[16,2,65536]{2,1,0:T(2,128)} %reshape.67, f32[16,10,65536]{2,1,0:T(8,128)} %reshape.68, f32[16,10]{1,0:T(8,128)S(1)} %bitcast.60, f32[10]{0:T(128)S(1)} %fusion.119, f32[16,10]{1,0:T(8,128)S(1)} %bitcast.59, f32[16,65536]{1,0:T(8,128)} %reduce_sum.180, ...), kind=kLoop, calls=%fused_computation.16 | loop fusion | flops 104857600 | bytes 75499440 | tf_op jit(solution)/shard_map/convert_element_type | solution.py:98
  368.0 31.0 %convert_element_type.110 = bf16[160,65536]{1,0:T(8,128)(2,1)} reshape(bf16[16,10,65536]{2,1,0:T(8,128)(2,1)} %get-tuple-element.35) | data formatting | bytes 41943040 | tf_op jit(solution)/shard_map/convert_element_type | solution.py:98
  399.1 25.9 %multiply_reduce_fusion.1 = (f32[160]{0:T(256)S(1)}, f32[160,384]{1,0:T(8,128)S(1)}) fusion(f32[160,384]{1,0:T(8,128)S(1)} %get-tuple-element.44, f32[160]{0:T(256)S(1)} %rsqrt.34, bf16[160,65536]{1,0:T(8,128)(2,1)} %convert_element_type.110, bf16[384,65536]{1,0:T(8,128)(2,1)} %param.24, f32[65536]{0:T(1024)S(1)} %rsqrt.35), kind=kOutput, calls=%fused_computation.142 | convolution fusion | flops 8128745472 | bytes 72058112 | tf_op jit(solution)/shard_map/rk,bk->rb/dot_general | solution.py:99
  425.0 0.1 fusion.153
  425.1 0.9 fusion.157
  426.0 0.4 copy-done.8
  426.4 8.9 fusion.60
  435.4 6.5 fusion.156
  441.9 2.4 fusion.114
  444.3 6.6 convolution_bitcast_fusion
  451.0 0.0 all-reduce.16.cloned.1.call-start
  451.0 42.7 %fusion.150 = f32[384,65536]{1,0:T(8,128)} fusion(bf16[160,65536]{1,0:T(8,128)(2,1)} %convert_element_type.110, f32[160,384]{1,0:T(8,128)S(1)} %get-tuple-element.44, f32[160]{0:T(256)S(1)} %rsqrt.34), kind=kOutput, calls=%fused_computation.222 | convolution fusion | flops 8053186560 | bytes 121881216 | tf_op jit(solution)/shard_map/rb,rk->bk/dot_general | solution.py:100
  493.8 33.3 %all-reduce.1 = (f32[]{:T(128)}, f32[2048]{0:T(1024)}, f32[2048]{0:T(1024)}, f32[384]{0:T(512)}) all-reduce(f32[]{:T(128)} %get-tuple-element.36, f32[2048]{0:T(1024)S(1)} %get-tuple-element.49, f32[2048]{0:T(1024)S(1)} %get-tuple-element.51, f32[384]{0:T(512)S(1)} %get-tuple-element.33), channel_id=1, replica_groups=mesh['vp'=2,'dp'=8] {'vp','dp'}, use_global_device_ids=true, to_apply=%region_24.25 | all-reduce | flops 4481 | bytes 35848 | tf_op jit(solution)/shard_map/psum | solution.py:96
  527.7 232.3 %all-reduce.18.cloned.1.call-done = (f32[1536,2048]{0,1:T(8,128)}, f32[2048,2048]{1,0:T(8,128)}, f32[2048,384]{1,0:T(8,128)}) async-done(((f32[1536,2048]{0,1:T(8,128)}, f32[2048,2048]{1,0:T(8,128)}, f32[2048,384]{1,0:T(8,128)}), (f32[1536,2048]{0,1:T(8,128)}, f32[2048,2048]{1,0:T(8,128)}, f32[2048,384]{1,0:T(8,128)})) %all-reduce.18.cloned.1.call-update) | async-done | bytes 32505872 | tf_op jit(solution)/shard_map/psum | solution.py:101
  760.1 12.6 copy.25
  772.7 1105.7 %all-reduce.16.cloned.1.call-done = f32[384,65536]{1,0:T(8,128)} async-done(((f32[384,65536]{1,0:T(8,128)}), f32[384,65536]{1,0:T(8,128)}) %all-reduce.16.cloned.1.call-update) | async-done | bytes 100663312 | tf_op jit(solution)/shard_map/psum | solution.py:100
  1878.3 45.1 %fusion.5 = f32[65536]{0:T(1024)S(1)} fusion(f32[384,65536]{1,0:T(8,128)} %all-reduce.16.cloned.1.call-done, bf16[384,65536]{1,0:T(8,128)(2,1)} %param.24, f32[65536]{0:T(1024)S(1)} %rsqrt.35), kind=kLoop, calls=%fused_computation.9 | loop fusion | flops 100597760 | bytes 151519232 | tf_op jit(solution)/shard_map/reduce_sum | solution.py:52
  1923.5 78.7 %fusion.7 = f32[384,65536]{1,0:T(8,128)} fusion(f32[384,65536]{1,0:T(8,128)} %all-reduce.16.cloned.1.call-done, bf16[384,65536]{1,0:T(8,128)(2,1)} %param.24, f32[65536]{0:T(1024)S(1)} %fusion.5, f32[65536]{0:T(1024)S(1)} %rsqrt.35), kind=kLoop, calls=%fused_computation.11 | loop fusion | flops 125829120 | bytes 252182528 | tf_op jit(solution)/shard_map/mul | solution.py:52
  2002.2 11.9 copy.33
  2014.2 1.7 copy.34
  2015.8 0.9 copy-done.1
  (41 shorter events, 0.3 us)
Async XLA Ops:
  7.2 125.8 %copy-start = (bf16[2048,384]{1,0:T(8,128)(2,1)S(1)}, bf16[2048,384]{1,0:T(8,128)(2,1)}, u32[]{:S(2)}) copy-start(bf16[2048,384]{1,0:T(8,128)(2,1)} %param.22) | copy-start | bytes 4718596
  7.2 140.3 %all-reduce.10.cloned.1.call-start = ((), (), s32[]{:S(2)}) async-start(), calls=%async_computation | async-start | bytes 524288 | tf_op jit(solution)/shard_map/psum | solution.py:80
  9.4 4.7 copy-start.12
  94.6 6.3 copy-start.9
  94.6 6.4 copy-start.10
  94.6 6.4 copy-start.11
  100.3 108.9 %all-reduce.12.cloned.1.call-start = ((), (), s32[]{:S(2)}) async-start(), calls=%async_computation.1 | async-start | bytes 524288 | tf_op jit(solution)/shard_map/psum | solution.py:80
  101.0 16.2 copy-start.2
  121.2 10.9 copy-start.7
  132.1 0.8 copy-start.5
  163.6 126.0 %all-reduce.14.cloned.1.call-start = ((), (), s32[]{:S(2)}) async-start(), calls=%async_computation.2 | async-start | bytes 524288 | tf_op jit(solution)/shard_map/psum | solution.py:80
  226.2 533.9 %all-reduce.18.cloned.1.call-start = ((), (), s32[]{:S(2)}) async-start(), calls=%async_computation.4 | async-start | bytes 65011712 | tf_op jit(solution)/shard_map/psum | solution.py:101
  399.1 26.0 %copy-start.13 = (f32[160,2048]{1,0:T(8,128)S(1)}, f32[160,2048]{1,0:T(8,128)}, u32[]{:S(2)}) copy-start(f32[160,2048]{1,0:T(8,128)} %get-tuple-element.42) | copy-start | bytes 3932164
  425.1 1.3 copy-start.8
  435.4 6.5 copy-start.6
  441.9 2.4 copy-start.3
  451.0 1427.3 %all-reduce.16.cloned.1.call-start = ((), (), s32[]{:S(2)}) async-start(), calls=%async_computation.3 | async-start | bytes 201326592 | tf_op jit(solution)/shard_map/psum | solution.py:100
  2002.2 12.0 copy-start.4
  2014.2 2.5 copy-start.1
Sparse Core Ops, SparseCore 0:
  100.5 47.0 all-reduce.9
  163.7 45.5 all-reduce.11
  226.3 45.5 all-reduce.13
  451.1 308.9 all-reduce.17
  764.3 1113.9 all-reduce.15
where the time goes:
time: 2030 us; the launch traced here: 2020 us
  waiting for transfers between devices  1360 us (67%)
  other arithmetic  268 us (13%)
  matrix products  174 us (9%)
  local copies, waits for them, and re-layouts  116 us (6%)
  blocking collectives  88.1 us (4%)
    psum x1, waiting for transfers between devices, local_step(): lax.psum(jnp.einsum('rb,rk->bk', s_emb, g_logits, preferred_element_type=...  1110 us
    psum x1, waiting for transfers between devices, local_step(): lax.psum(mlp_backward(g_emb, student_x, saved, w_mid, w_out), ('vp', 'dp'))  232 us
    mul x1, other arithmetic, col_normalize_backward(): (g_unit - unit * jnp.sum(unit * g_unit, axis=0, keepdims=True)) * inv_col  78.7 us
    reshape x1, local copies, waits for them, and re-layouts, local_step(): logits = logits.reshape(n_img, ALL_CROPS, local_proto)  46.5 us
    reduce_sum x1, other arithmetic, col_normalize_backward(): jnp.sum(unit * g_unit, axis=0, keepdims=True)  45.1 us
    dot_general x1, matrix products, local_step(): jnp.einsum('rb,rk->bk', s_emb, g_logits, preferred_element_type=jnp.float32)  42.7 us
  transfers between devices with their start and end apart: 5, of which 4 were waited for; matrix products, arithmetic and copies ran while one was open for 9% of the time, Pallas kernels for 0%

commit v1 on v0

v1 whole, which is shorter than its diff:
```python
import functools

import jax
import jax.numpy as jnp
from jax import lax
from jax.experimental import pallas as pl
from jax.experimental.pallas import tpu as pltpu
from jax.sharding import PartitionSpec as P

ALL_CROPS = 10
GLOBAL_CROPS = 2
TEMP_STUDENT = 0.1
TEMP_TEACHER = 0.04
LOG2E = 1.4426950408889634
LANES = 128
NB_A = 512
NB_B = 512
OUT_SLOTS = 4
F32 = jnp.float32
BF16 = jnp.bfloat16
MESH = pl.DeviceIdType.MESH
HBM = pl.BlockSpec(memory_space=pl.ANY)
VMEM = pl.BlockSpec(memory_space=pltpu.VMEM)


def gelu_slope(pre):
    cdf = 0.5 * (1.0 + lax.erf(pre * 0.7071067811865476))
    return cdf + pre * jnp.exp(-0.5 * pre * pre) * 0.3989422804014327


def mlp_forward(feats, w_in, b_in, w_mid, b_mid, w_out, b_out):
    pre_one = jnp.dot(feats, w_in, preferred_element_type=F32) + b_in.astype(F32)
    hid_one = jax.nn.gelu(pre_one, approximate=False).astype(BF16)
    pre_two = jnp.dot(hid_one, w_mid, preferred_element_type=F32) + b_mid.astype(F32)
    hid_two = jax.nn.gelu(pre_two, approximate=False).astype(BF16)
    proj = jnp.dot(hid_two, w_out, preferred_element_type=F32) + b_out.astype(F32)
    inv_norm = lax.rsqrt(jnp.sum(proj * proj, axis=-1, keepdims=True))
    unit = proj * inv_norm
    return unit, (pre_one, hid_one, pre_two, hid_two, unit, inv_norm)


def mlp_backward(g_emb, feats, saved, w_mid, w_out):
    pre_one, hid_one, pre_two, hid_two, unit, inv_norm = saved
    g_proj = (g_emb - unit * jnp.sum(unit * g_emb, axis=-1, keepdims=True)) * inv_norm
    g_proj_lo = g_proj.astype(BF16)
    g_w_out = jnp.einsum('nh,nb->hb', hid_two, g_proj_lo, preferred_element_type=F32)
    g_hid_two = jnp.einsum('nb,hb->nh', g_proj_lo, w_out, preferred_element_type=F32)
    g_pre_two = g_hid_two.astype(BF16).astype(F32) * gelu_slope(pre_two)
    g_pre_two_lo = g_pre_two.astype(BF16)
    g_w_mid = jnp.einsum('ng,nh->gh', hid_one, g_pre_two_lo, preferred_element_type=F32)
    g_hid_one = jnp.einsum('nh,gh->ng', g_pre_two_lo, w_mid, preferred_element_type=F32)
    g_pre_one = g_hid_one.astype(BF16).astype(F32) * gelu_slope(pre_one)
    g_w_in = jnp.einsum('nf,nh->fh', feats, g_pre_one.astype(BF16), preferred_element_type=F32)
    return (g_w_in, jnp.sum(g_pre_one, axis=0), g_w_mid, jnp.sum(g_pre_two, axis=0), g_w_out, jnp.sum(g_proj, axis=0))


def unit_columns(block):
    block_f = block.astype(F32)
    inv_col = lax.rsqrt(jnp.sum(block_f * block_f, axis=0, keepdims=True))
    return block_f * inv_col, inv_col


def dot(left, right):
    return jnp.dot(left, right, preferred_element_type=F32)


def dot_t(left, right):
    return lax.dot_general(left, right, (((1,), (1,)), ((), ())), preferred_element_type=F32)


def to_column(row):
    return jnp.transpose(jnp.broadcast_to(row, (LANES, row.shape[1])))


def to_row(acc):
    return jnp.sum(jnp.transpose(acc), axis=0, keepdims=True)


def fold_lanes(wide):
    total = wide[:, :LANES]
    for start in range(LANES, wide.shape[1], LANES):
        total = total + wide[:, start:start + LANES]
    return total


def my_place():
    return lax.axis_index('vp'), lax.axis_index('dp')


def gather_kernel(n_dp, block_ref, all_ref, out_sem, in_sem, fwd_out, fwd_in):
    vp, me = my_place()
    n_chip = n_dp // 2
    chip, core = me // 2, me % 2
    partner = chip * 2 + 1 - core
    barrier = pltpu.get_barrier_semaphore()
    pl.semaphore_signal(barrier, inc=1, device_id=(vp, partner), device_id_type=MESH)
    for k in range(1, n_chip):
        peer = ((chip + k) % n_chip) * 2 + core
        pl.semaphore_signal(barrier, inc=1, device_id=(vp, peer), device_id_type=MESH)
    pl.semaphore_wait(barrier, n_chip)
    sends = []
    for k in range(1, n_chip):
        peer = ((chip + k) % n_chip) * 2 + core
        sends.append(pltpu.make_async_remote_copy(
            src_ref=block_ref, dst_ref=all_ref.at[me], send_sem=out_sem.at[k], recv_sem=in_sem.at[chip],
            device_id=(vp, peer), device_id_type=MESH))
    own = pltpu.make_async_remote_copy(
        src_ref=block_ref, dst_ref=all_ref.at[me], send_sem=fwd_out.at[chip], recv_sem=fwd_in.at[chip],
        device_id=(vp, partner), device_id_type=MESH)
    for copy in sends:
        copy.start()
    own.start()
    all_ref[me] = block_ref[...]
    for k in range(1, n_chip):
        src = (chip + n_chip - k) % n_chip
        slot = src * 2 + core
        peer_copy = pltpu.make_async_remote_copy(
            src_ref=block_ref, dst_ref=all_ref.at[slot], send_sem=out_sem.at[k], recv_sem=in_sem.at[src],
            device_id=(vp, partner), device_id_type=MESH)
        peer_copy.wait_recv()
        forward = pltpu.make_async_remote_copy(
            src_ref=all_ref.at[slot], dst_ref=all_ref.at[slot], send_sem=fwd_out.at[src], recv_sem=fwd_in.at[src],
            device_id=(vp, partner), device_id_type=MESH)
        forward.start()
    for copy in sends:
        copy.wait_send()
    for src in range(n_chip):
        slot = src * 2 + core
        other = src * 2 + 1 - core
        pltpu.make_async_remote_copy(
            src_ref=all_ref.at[slot], dst_ref=all_ref.at[other], send_sem=fwd_out.at[src], recv_sem=fwd_in.at[src],
            device_id=(vp, partner), device_id_type=MESH).wait()


def gather_dp(block, n_dp, collective_id):
    return pl.pallas_call(
        functools.partial(gather_kernel, n_dp),
        out_shape=jax.ShapeDtypeStruct((n_dp,) + block.shape, block.dtype),
        in_specs=[VMEM],
        out_specs=VMEM,
        scratch_shapes=[pltpu.SemaphoreType.DMA((n_dp // 2,))] * 4,
        compiler_params=pltpu.CompilerParams(
            collective_id=collective_id, has_side_effects=True, vmem_limit_bytes=48 << 20),
        name="gather_dp",
    )(block)


def stats_kernel(n_vp, n_dp, zs_ref, zt_ref, v_hbm, vt_hbm, c_ref, rs_ref, r_ref, ge_ref, loss_ref,
                 vbuf, tbuf, in_sem, ubuf, kbuf, acc_s, acc_r, wbuf, snd, rcv, send_sem, recv_sem, c_out, c_in):
    vp, dp = my_place()
    n_dev = n_vp * n_dp
    me = vp * n_dp + dp
    rows, rows_t = zs_ref.shape[0], zt_ref.shape[0]
    n_img = rows // ALL_CROPS
    n_col = kbuf.shape[1]
    n_blk = n_col // NB_A
    base = dp * n_col

    barrier = pltpu.get_barrier_semaphore()
    for k in range(1, n_dev):
        peer = (me + k) % n_dev
        pl.semaphore_signal(barrier, inc=1, device_id=(peer // n_dp, peer % n_dp), device_id_type=MESH)

    def load(j, slot):
        cols = pl.ds(pl.multiple_of(base + j * NB_A, NB_A), NB_A)
        return (pltpu.make_async_copy(v_hbm.at[:, cols], vbuf.at[slot], in_sem.at[0, slot]),
                pltpu.make_async_copy(vt_hbm.at[:, cols], tbuf.at[slot], in_sem.at[1, slot]))

    for copy in load(0, 0):
        copy.start()
    acc_s[...] = jnp.zeros_like(acc_s)
    acc_r[...] = jnp.zeros_like(acc_r)
    ge_ref[...] = jnp.zeros_like(ge_ref)

    @pl.loop(0, n_blk)
    def _(j):
        slot = j % 2

        @pl.when(j + 1 < n_blk)
        def _():
            for copy in load(j + 1, 1 - slot):
                copy.start()

        for copy in load(j, slot):
            copy.wait()
        here = pl.ds(pl.multiple_of(j * NB_A, NB_A), NB_A)
        unit_t = unit_columns(tbuf[slot])[0].astype(BF16)
        kern = jnp.exp2(dot(zt_ref[...], unit_t) * (LOG2E / TEMP_TEACHER))
        kbuf[:, here] = kern
        acc_r[...] += fold_lanes(kern * (1.0 / jnp.sum(kern, axis=0, keepdims=True)))
        unit = unit_columns(vbuf[slot])[0].astype(BF16)
        ubuf[:, here] = unit
        exp_s = jnp.exp2(dot(zs_ref[...], unit) * (LOG2E / TEMP_STUDENT))
        acc_s[...] += fold_lanes(exp_s)
        ge_ref[...] += dot_t(exp_s.astype(BF16), unit)

    pl.semaphore_wait(barrier, n_dev - 1)

    def exchange(step, width):
        def copy(k, dst, peer):
            return pltpu.make_async_remote_copy(
                src_ref=snd.at[step, :, :width], dst_ref=rcv.at[step, dst, :, :width],
                send_sem=send_sem.at[step, k], recv_sem=recv_sem.at[step, dst],
                device_id=(peer // n_dp, peer % n_dp), device_id_type=MESH)
        for k in range(1, n_dev):
            copy(k, me, (me + k) % n_dev).start()
        rcv[step, me, :, :width] = snd[step, :, :width]
        for k in range(1, n_dev):
            src = (me + n_dev - k) % n_dev
            copy(k, src, src).wait()
        total = rcv[step, 0, :, :width]
        for k in range(1, n_dev):
            total = total + rcv[step, k, :, :width]
        return total

    snd[0, :, :rows_t] = to_row(acc_r[...])
    snd[0, :, rows_t:rows_t + rows] = to_row(acc_s[...])
    total = exchange(0, rows_t + rows)
    row_sum = total[:, rows_t:]
    rs_ref[...] = row_sum
    r_row = 1.0 / total[:, :rows_t]

    for step in (1, 2):
        r_col = to_column(r_row)
        acc_r[...] = jnp.zeros_like(acc_r)

        @pl.loop(0, n_col // LANES)
        def _(j):
            here = pl.ds(pl.multiple_of(j * LANES, LANES), LANES)
            kern = kbuf[:, here]
            c_row = 1.0 / jnp.sum(kern * r_col, axis=0, keepdims=True)
            acc_r[...] += kern * c_row
            if step == 2:
                c_ref[dp, :, here] = c_row

        if step == 2:
            for k in range(1, n_dp):
                pltpu.make_async_remote_copy(
                    src_ref=c_ref.at[dp], dst_ref=c_ref.at[dp], send_sem=c_out.at[k], recv_sem=c_in.at[dp],
                    device_id=(vp, (dp + k) % n_dp), device_id_type=MESH).start()
        snd[step, :, :rows_t] = to_row(acc_r[...])
        r_row = 1.0 / exchange(step, rows_t)
    r_ref[...] = r_row

    r_col = to_column(r_row)
    r_wide = jnp.concatenate([r_col] * (NB_A // LANES), axis=1)
    wbuf[...] = jnp.zeros_like(wbuf)

    @pl.loop(0, n_blk)
    def _(j):
        here = pl.ds(pl.multiple_of(j * NB_A, NB_A), NB_A)
        q_mat = kbuf[:, here] * c_ref[dp, :, here] * r_wide
        q_hi = q_mat.astype(BF16)
        q_lo = (q_mat - q_hi.astype(F32)).astype(BF16)
        unit = ubuf[:, here]
        wbuf[...] += dot_t(q_hi, unit) + dot_t(q_lo, unit)

    w_zero = wbuf[:n_img]
    w_one = wbuf[n_img:]
    w_both = w_zero + w_one
    scale = 1.0 / (n_img * GLOBAL_CROPS * (ALL_CROPS - 1))
    log_rs = jnp.log(row_sum)
    inv_rs = to_column(1.0 / row_sum)
    loss = jnp.zeros((1, LANES), F32)
    for v in range(ALL_CROPS):
        block = pl.ds(v * n_img, n_img)
        count = float(GLOBAL_CROPS - (v < GLOBAL_CROPS))
        w_v = (w_one, w_zero)[v] if v < GLOBAL_CROPS else w_both
        inv = inv_rs[v * n_img:(v + 1) * n_img]
        inv = jnp.concatenate([inv] * (ge_ref.shape[1] // LANES), axis=1)
        dots = fold_lanes(jnp.sum(zs_ref[block].astype(F32) * w_v, axis=0, keepdims=True))
        logs = log_rs[:, v * n_img:(v + 1) * n_img]
        loss += (count / n_dev) * logs - (1.0 / TEMP_STUDENT) * dots
        ge_ref[block] = (count * (ge_ref[block] * inv) - w_v) * (scale / TEMP_STUDENT)
    loss_ref[...] = loss * scale

    for k in range(1, n_dp):
        src = (dp + n_dp - k) % n_dp
        pltpu.make_async_remote_copy(
            src_ref=c_ref.at[dp], dst_ref=c_ref.at[src], send_sem=c_out.at[k], recv_sem=c_in.at[src],
            device_id=(vp, src), device_id_type=MESH).wait()


def sinkhorn_stats(z_s, z_t, protos, ema_protos, n_vp, n_dp):
    rows, width = z_s.shape
    rows_t = z_t.shape[0]
    n_col = protos.shape[1] // n_dp
    n_dev = n_vp * n_dp
    flops = 2 * rows * n_col * width * 2
    return pl.pallas_call(
        functools.partial(stats_kernel, n_vp, n_dp),
        out_shape=(jax.ShapeDtypeStruct((n_dp, 1, n_col), F32),
                   jax.ShapeDtypeStruct((1, rows), F32),
                   jax.ShapeDtypeStruct((1, rows_t), F32),
                   jax.ShapeDtypeStruct((rows, width), F32),
                   jax.ShapeDtypeStruct((1, LANES), F32)),
        in_specs=[VMEM, VMEM, HBM, HBM],
        out_specs=(VMEM,) * 5,
        scratch_shapes=[
            pltpu.VMEM((2, width, NB_A), BF16),
            pltpu.VMEM((2, width, NB_A), BF16),
            pltpu.SemaphoreType.DMA((2, 2)),
            pltpu.VMEM((width, n_col), BF16),
            pltpu.VMEM((rows_t, n_col), F32),
            pltpu.VMEM((rows, LANES), F32),
            pltpu.VMEM((rows_t, LANES), F32),
            pltpu.VMEM((rows_t, width), F32),
            pltpu.VMEM((3, 1, rows + rows_t), F32),
            pltpu.VMEM((3, n_dev, 1, rows + rows_t), F32),
            pltpu.SemaphoreType.DMA((3, n_dev)),
            pltpu.SemaphoreType.DMA((3, n_dev)),
            pltpu.SemaphoreType.DMA((n_dp,)),
            pltpu.SemaphoreType.DMA((n_dp,)),
        ],
        compiler_params=pltpu.CompilerParams(
            collective_id=1, has_side_effects=True, vmem_limit_bytes=60 << 20),
        cost_estimate=pl.CostEstimate(flops=flops, bytes_accessed=4 * width * n_col, transcendentals=rows * n_col),
        name="sinkhorn_stats",
    )(z_s, z_t, protos, ema_protos)


def grads_kernel(zs_ref, zst_ref, zt_ref, rs_ref, r_ref, c_ref, v_hbm, vt_hbm, g_hbm,
                 vbuf, tbuf, obuf, in_sem, loc_sem, out_sem, recv_sem):
    vp, dp = my_place()
    chip, core = dp // 2, dp % 2
    partner = chip * 2 + 1 - core
    rows, rows_t = zs_ref.shape[0], zt_ref.shape[0]
    n_img = rows // ALL_CROPS
    half = v_hbm.shape[1] // 2
    n_slice = c_ref.shape[2]
    n_blk = half // NB_B
    base = core * half
    barrier = pltpu.get_barrier_semaphore()
    pl.semaphore_signal(barrier, inc=1, device_id=(vp, partner), device_id_type=MESH)

    def load(j, slot):
        cols = pl.ds(pl.multiple_of(base + j * NB_B, NB_B), NB_B)
        return (pltpu.make_async_copy(v_hbm.at[:, cols], vbuf.at[slot], in_sem.at[0, slot]),
                pltpu.make_async_copy(vt_hbm.at[:, cols], tbuf.at[slot], in_sem.at[1, slot]))

    def store(j):
        slot = j % OUT_SLOTS
        cols = pl.ds(pl.multiple_of(base + j * NB_B, NB_B), NB_B)
        return (pltpu.make_async_copy(obuf.at[slot], g_hbm.at[:, cols], loc_sem.at[slot]),
                pltpu.make_async_remote_copy(
                    src_ref=obuf.at[slot], dst_ref=g_hbm.at[:, cols], send_sem=out_sem.at[slot],
                    recv_sem=recv_sem.at[j], device_id=(vp, partner), device_id_type=MESH))

    def finish(j):
        local, remote = store(j)
        local.wait()
        remote.wait_send()

    for copy in load(0, 0):
        copy.start()
    scale = 1.0 / (n_img * GLOBAL_CROPS * (ALL_CROPS - 1)) / TEMP_STUDENT
    lanes = lax.broadcasted_iota(jnp.int32, (1, rows), 1)
    weight = jnp.where(lanes < GLOBAL_CROPS * n_img, scale, GLOBAL_CROPS * scale)
    bias = to_column(jnp.log(weight / rs_ref[...]) * LOG2E)
    bias = jnp.concatenate([bias] * (NB_B // LANES), axis=1)
    r_col = to_column(r_ref[...] * scale)
    r_wide = jnp.concatenate([r_col] * (NB_B // LANES), axis=1)
    pl.semaphore_wait(barrier, 1)

    @pl.loop(0, n_blk)
    def _(j):
        slot = j % 2

        @pl.when(j + 1 < n_blk)
        def _():
            for copy in load(j + 1, 1 - slot):
                copy.start()

        @pl.when(j >= 1)
        def _():
            for copy in store(j - 1):
                copy.start()

        @pl.when(j >= OUT_SLOTS)
        def _():
            finish(j - OUT_SLOTS)

        for copy in load(j, slot):
            copy.wait()
        unit_t = unit_columns(tbuf[slot])[0].astype(BF16)
        col = base + j * NB_B
        c_row = c_ref[col // n_slice, :, pl.ds(pl.multiple_of(col % n_slice, NB_B), NB_B)]
        q_mat = jnp.exp2(dot(zt_ref[...], unit_t) * (LOG2E / TEMP_TEACHER)) * c_row * r_wide
        q_zero, q_one = q_mat[:n_img], q_mat[n_img:]
        q_both = q_zero + q_one
        unit, inv_col = unit_columns(vbuf[slot])
        logits = dot(zs_ref[...], unit.astype(BF16))
        soft = jnp.exp2(logits * (LOG2E / TEMP_STUDENT) + bias)
        target = jnp.concatenate([q_one, q_zero] + [q_both] * (ALL_CROPS - GLOBAL_CROPS), axis=0)
        g_unit = dot(zst_ref[...], (soft - target).astype(BF16))
        obuf[j % OUT_SLOTS] = (g_unit - unit * jnp.sum(unit * g_unit, axis=0, keepdims=True)) * inv_col

    for copy in store(n_blk - 1):
        copy.start()
    for j in range(n_blk - OUT_SLOTS, n_blk):
        finish(j)

    @pl.loop(0, n_blk)
    def _(j):
        store(j)[1].wait_recv()


def proto_grads(z_s, z_t, row_sum, r_row, c_all, protos, ema_protos):
    rows, width = z_s.shape
    rows_t = z_t.shape[0]
    n_col = protos.shape[1]
    n_blk = n_col // 2 // NB_B
    return pl.pallas_call(
        grads_kernel,
        out_shape=jax.ShapeDtypeStruct((width, n_col), F32),
        in_specs=[VMEM] * 6 + [HBM] * 2,
        out_specs=HBM,
        scratch_shapes=[
            pltpu.VMEM((2, width, NB_B), BF16),
            pltpu.VMEM((2, width, NB_B), BF16),
            pltpu.VMEM((OUT_SLOTS, width, NB_B), F32),
            pltpu.SemaphoreType.DMA((2, 2)),
            pltpu.SemaphoreType.DMA((OUT_SLOTS,)),
            pltpu.SemaphoreType.DMA((OUT_SLOTS,)),
            pltpu.SemaphoreType.DMA((n_blk,)),
        ],
        compiler_params=pltpu.CompilerParams(
            collective_id=2, has_side_effects=True, vmem_limit_bytes=60 << 20),
        cost_estimate=pl.CostEstimate(
            flops=2 * rows * n_col * width, bytes_accessed=4 * width * n_col, transcendentals=rows * n_col // 2),
        name="proto_grads",
    )(z_s, z_s.T, z_t, row_sum, r_row, c_all, protos, ema_protos)


def solution(mesh):
    n_vp = mesh.shape['vp']
    n_dp = mesh.shape['dp']

    def local_step(student_x, teacher_x, w_in, b_in, w_mid, b_mid, w_out, b_out, protos,
                   ema_w_in, ema_b_in, ema_w_mid, ema_b_mid, ema_w_out, ema_b_out, ema_protos):
        rows, feat = student_x.shape
        n_img = rows // ALL_CROPS
        width = protos.shape[0]
        total_img = n_img * n_dp
        t_emb = mlp_forward(teacher_x, ema_w_in, ema_b_in, ema_w_mid, ema_b_mid, ema_w_out, ema_b_out)[0]
        s_emb = mlp_forward(student_x, w_in, b_in, w_mid, b_mid, w_out, b_out)[0]
        z_all = gather_dp(jnp.concatenate([s_emb, t_emb], axis=0), n_dp, 0)
        z_s = z_all[:, :rows].reshape(total_img, ALL_CROPS, width).transpose(1, 0, 2).reshape(-1, width).astype(BF16)
        z_t = z_all[:, rows:].reshape(total_img, GLOBAL_CROPS, width).transpose(1, 0, 2).reshape(-1, width).astype(BF16)
        c_all, row_sum, r_row, g_emb, loss = sinkhorn_stats(z_s, z_t, protos, ema_protos, n_vp, n_dp)
        g_protos = proto_grads(z_s, z_t, row_sum, r_row, c_all, protos, ema_protos)
        g_emb, loss = lax.psum((g_emb, loss), ('vp', 'dp'))
        x_all = gather_dp(student_x.astype(F32), n_dp, 3).reshape(n_dp * rows, feat).astype(BF16)
        g_emb = g_emb.reshape(ALL_CROPS, total_img, width).transpose(1, 0, 2).reshape(-1, width)
        saved = mlp_forward(x_all, w_in, b_in, w_mid, b_mid, w_out, b_out)[1]
        head_grads = mlp_backward(g_emb, x_all, saved, w_mid, w_out)
        return (jnp.sum(loss),) + tuple(head_grads) + (g_protos,)

    by_rows = P('dp', None)
    by_cols = P(None, 'vp')
    replicated = P()
    head_specs = (replicated,) * 6
    in_specs = (by_rows, by_rows) + head_specs + (by_cols,) + head_specs + (by_cols,)
    out_specs = (replicated,) * 7 + (by_cols,)
    return jax.shard_map(local_step, mesh=mesh, in_specs=in_specs, out_specs=out_specs, check_vma=False)
```

time: 2030 us -> 590 us (0.29)
  waiting for transfers between devices: 1360 us -> 0.02 us
  Pallas kernels: 0 us -> 267 us
  other arithmetic: 268 us -> 10.7 us
  blocking collectives: 88.1 us -> 31.3 us
    psum x5 -> x1, waiting for transfers between devices: 1360 us -> 0.01 us  [local_step(): g_emb, loss = lax.psum((g_emb, loss), ('vp', 'dp'))]
    pallas_call x0 -> x4, Pallas kernels: none -> 267 us  [the longest x1 123 us: proto_grads(): pl.pallas_call(grads_kernel, out_shape=jax.ShapeDtypeStruct((width, n_col...]
    reduce_sum x11 -> x2, other arithmetic: 139 us -> 3.18 us  [the longest x1 1.92 us: mlp_backward(): jnp.sum(unit * g_emb, axis=-1, keepdims=True)]
    mul x4 -> x2, other arithmetic: 87.8 us -> 0.17 us  [mlp_forward(): unit = proj * inv_norm]
    psum x5 -> x1, blocking collectives: 83.1 us -> 31.3 us  [local_step(): g_emb, loss = lax.psum((g_emb, loss), ('vp', 'dp'))]
    unnamed x31 -> x56, local copies, waits for them, and re-layouts: 28.4 us -> 78.3 us
    reshape x2 -> x3, local copies, waits for them, and re-layouts: 55.8 us -> 10.9 us  [local_step(): g_emb.reshape(ALL_CROPS, total_img, width).transpose(1, 0, 2)]
    convert_element_type x8, other arithmetic: 40.2 us -> 6.17 us  [the longest x1 3.89 us: local_step(): gather_dp(student_x.astype(F32), n_dp, 3).reshape(n_dp * rows, feat)]
  transfers between devices with their start and end apart: 5 -> 1, of which waited for: 4 -> 0; matrix products, arithmetic and copies ran while one was open for 9% -> 14% of each run, Pallas kernels for 0% -> 31%
where the time goes in v1:
time: 590 us; the launch traced here: 581 us
  Pallas kernels  267 us (45%)
  matrix products  161 us (27%)
  local copies, waits for them, and re-layouts  95.9 us (16%)
  blocking collectives  31.3 us (5%)
  between operations  14.9 us (3%)
  other arithmetic  10.7 us (2%)
    pallas_call x1, Pallas kernels, proto_grads(): pl.pallas_call(grads_kernel, out_shape=jax.ShapeDtypeStruct((width, n_col...  123 us
    pallas_call x2, Pallas kernels, gather_dp(): pl.pallas_call(functools.partial(gather_kernel, n_dp), out_shape=jax.Shap...  78.3 us
    unnamed x56, local copies, waits for them, and re-layouts  78.3 us
    pallas_call x1, Pallas kernels, sinkhorn_stats(): pl.pallas_call(functools.partial(stats_kernel, n_vp, n_dp), out_shape=(ja...  65.8 us
    dot_general x2, matrix products, mlp_forward(): jnp.dot(hid_one, w_mid, preferred_element_type=F32) + b_mid.astype(F32)  49.6 us
    dot_general x2, matrix products, mlp_forward(): jnp.dot(feats, w_in, preferred_element_type=F32) + b_in.astype(F32)  37.2 us
    psum x1, blocking collectives, local_step(): g_emb, loss = lax.psum((g_emb, loss), ('vp', 'dp'))  31.3 us
    dot_general x1, matrix products, mlp_backward(): jnp.einsum('nh,gh->ng', g_pre_two_lo, w_mid, preferred_element_type=F32)  21.2 us
  transfers between devices with their start and end apart: 1, of which 0 were waited for; matrix products, arithmetic and copies ran while one was open for 14% of the time, Pallas kernels for 31%

profile of v1, /device:TPU:0, one launch (start us, length us, event | category | flops | bytes accessed | tf_op | source)
XLA Modules:
  0.0 581.4 jit_solution(16821664969582968195)
XLA Ops:
  7.2 0.0 copy-start
  7.2 0.0 all-reduce.2.cloned.1.call-start
  7.2 0.8 convert_element_type.83
  8.0 0.7 convert_element_type.85
  8.7 0.7 convert_element_type.87
  9.4 0.0 copy-done.9
  9.4 0.0 copy-start.15
  9.4 0.0 copy-start.16
  9.5 13.6 %fusion.39 = bf16[160,2048]{1,0:T(8,128)(2,1)S(1)} fusion(bf16[2048,2048]{1,0:T(8,128)(2,1)} %param.20, bf16[160,1536]{1,0:T(8,128)(2,1)} %param.16, bf16[1536,2048]{1,0:T(8,128)(2,1)} %param.18, f32[2048]{0:T(1024)S(1)} %convert_element_type.85, f32[2048]{0:T(1024)S(1)} %convert_element_type.83), kind=kOutput, calls=%fused_computation.73 | convolution fusion | flops 2392064000 | bytes 15843328 | tf_op jit(solution)/shard_map/dot_general | solution.py:34
  23.1 0.0 copy-done.11
  23.1 0.0 copy-done
  23.1 0.6 multiply_reduce_fusion.2
  23.7 0.0 copy-done.13
  23.8 0.0 copy-done.14
  23.8 0.0 copy-done.15
  23.8 0.0 copy-done.16
  23.8 4.5 fusion.92
  28.3 6.0 %multiply_reduce_fusion.3 = (f32[32]{0:T(128)S(1)}, f32[32,384]{1,0:T(8,128)S(1)}) fusion(f32[384]{0:T(512)S(1)} %convert_element_type.92, bf16[2048,384]{1,0:T(8,128)(2,1)} %param.29, bf16[32,2048]{1,0:T(8,128)(2,1)S(1)} %fusion.92, bf16[2048,2048]{1,0:T(8,128)(2,1)} %param.27, f32[2048]{0:T(1024)S(1)} %convert_element_type.90), kind=kOutput, calls=%fused_computation.211 | convolution fusion | flops 323129312 | bytes 10151552 | tf_op jit(solution)/shard_map/dot_general | solution.py:36
  34.3 0.1 broadcast_multiply_fusion
  34.4 0.1 broadcast_multiply_fusion.1
  34.5 19.4 %gather_dp.2 = f32[8,192,384]{2,1,0:T(8,128)S(1)} custom-call(f32[192,384]{1,0:T(8,128)S(1)} %pad_maximum_fusion.block_ref), custom_call_target="tpu_custom_call" | custom-call | tf_op jit(solution)/shard_map/gather_dp/pallas_call | solution.py:136
  53.9 0.1 convert.4
  54.1 0.0 copy-start.3
  54.1 1.1 slice.10
  55.2 0.2 copy-done.3
  55.4 2.2 convert_element_type.93
  57.6 1.2 copy.30
  58.8 0.0 slice-done
  58.8 0.1 convert_element_type.96
  58.9 0.7 copy.31
  59.6 65.8 %sinkhorn_stats.1 = (f32[8,1,8192]{2,1,0:T(1,128)}, f32[1,1280]{1,0:T(1,128)}, f32[1,256]{1,0:T(1,128)}, f32[1280,384]{1,0:T(8,128)}, f32[1,128]{1,0:T(1,128)}) custom-call(bf16[1280,384]{1,0:T(8,128)(2,1)} %bitcast.40, bf16[256,384]{1,0:T(8,128)(2,1)} %bitcast.48, bf16[384,65536]{1,0:T(8,128)(2,1)} %v_hbm.3, bf16[384,65536]{1,0:T(8,128)(2,1)} %vt_hbm.3), custom_call_target="tpu_custom_call" | custom-call | flops 16106127360 | bytes 12582912 | tf_op jit(solution)/shard_map/sinkhorn_stats/pallas_call | solution.py:290
  125.3 4.4 copy.37
  129.8 3.7 reshape.52
  133.4 2.8 copy.33
  136.3 0.0 all-reduce.2.cloned.1.call-update
  136.3 1.4 copy.34
  137.7 0.1 convert_element_type.99.block_ref
  137.8 0.0 slice-start.3
  137.8 58.9 %gather_dp.3 = f32[8,160,1536]{2,1,0:T(8,128)} custom-call(f32[160,1536]{1,0:T(8,128)S(1)} %convert_element_type.99.block_ref), custom_call_target="tpu_custom_call" | custom-call | tf_op jit(solution)/shard_map/gather_dp/pallas_call | solution.py:136
  196.7 0.0 slice-start.4
  196.7 0.0 slice-start.1
  196.8 3.9 convert_element_type.100
  200.7 0.0 copy-start.10
  200.7 0.0 slice-start.2
  200.7 32.7 %fusion.2 = (bf16[1280,2048]{1,0:T(8,128)(2,1)S(1)}, f32[1280,2048]{1,0:T(8,128)}) fusion(f32[2048]{0:T(1024)S(1)} %convert_element_type.83, bf16[1280,1536]{1,0:T(8,128)(2,1)S(1)} %bitcast.44, bf16[1536,2048]{1,0:T(8,128)(2,1)S(1)} %bitcast.53), kind=kOutput, calls=%fused_computation.6 | convolution fusion | flops 8226078720 | bytes 25960448 | tf_op jit(solution)/shard_map/dot_general | solution.py:32
  233.4 36.0 %fusion.5 = (bf16[1280,2048]{1,0:T(8,128)(2,1)}, f32[1280,2048]{1,0:T(8,128)}) fusion(f32[2048]{0:T(1024)S(1)} %copy-done.10, bf16[1280,2048]{1,0:T(8,128)(2,1)S(1)} %get-tuple-element.40, bf16[2048,2048]{1,0:T(8,128)(2,1)S(1)} %bitcast.51), kind=kOutput, calls=%fused_computation.9 | convolution fusion | flops 10910433280 | bytes 29368320 | tf_op jit(solution)/shard_map/dot_general | solution.py:34
  269.4 0.0 copy-start.12
  269.4 123.2 %proto_grads.1 = f32[384,65536]{1,0:T(8,128)} custom-call(bf16[1280,384]{1,0:T(8,128)(2,1)} %bitcast.41, bf16[384,1280]{1,0:T(8,128)(2,1)} %bitcast.47, bf16[256,384]{1,0:T(8,128)(2,1)} %bitcast.49, f32[1,1280]{1,0:T(1,128)} %get-tuple-element.15.rs_ref, f32[1,256]{1,0:T(1,128)} %get-tuple-element.16.r_ref, f32[8,1,8192]{2,1,0:T(1,128)} %get-tuple-element.17.c_ref, ...), custom_call_target="tpu_custom_call" | custom-call | flops 64424509440 | bytes 100663296 | tf_op jit(solution)/shard_map/proto_grads/pallas_call | solution.py:413
  392.6 4.8 multiply_reduce_fusion.1
  397.4 31.3 %psum.14 = f32[1,128]{1,0:T(1,128)} all-reduce(f32[1,128]{1,0:T(1,128)} %get-tuple-element.13), channel_id=1, replica_groups=mesh['vp'=2,'dp'=8] {'vp','dp'}, use_global_device_ids=true, to_apply=%region_2.0 | all-reduce | flops 128 | bytes 1024 | tf_op jit(solution)/shard_map/psum | solution.py:452
  428.7 1.3 reduce_sum.74
  430.0 1.9 multiply_reduce_fusion
  431.9 0.2 copy-done.2
  432.1 1.1 fusion.88
  433.2 7.5 %fusion.203 = f32[2048,384]{1,0:T(8,128)} fusion(bf16[1280,2048]{1,0:T(8,128)(2,1)} %get-tuple-element.42, bf16[1280,384]{0,1:T(8,128)(2,1)S(1)} %get-tuple-element.35), kind=kOutput, calls=%fused_computation.275 | convolution fusion | flops 2013265920 | bytes 9371648 | tf_op jit(solution)/shard_map/nh,nb->hb/dot_general | solution.py:46
  440.7 0.0 slice-done.6
  440.7 0.0 slice-start.9
  440.7 7.2 %fusion.202 = (f32[2048]{0:T(1024)}, bf16[1280,2048]{1,0:T(8,128)(2,1)S(1)}) fusion(f32[1280,2048]{1,0:T(8,128)S(1)} %bitcast.55, f32[2048]{0:T(1024)S(1)} %copy-done.10, bf16[1280,384]{0,1:T(8,128)(2,1)S(1)} %get-tuple-element.35, bf16[2048,384]{1,0:T(8,128)(2,1)S(1)} %copy-done), kind=kOutput, calls=%fused_computation.274 | convolution fusion | flops 2049964032 | bytes 18300928 | tf_op jit(solution)/shard_map/nb,hb->nh/dot_general | solution.py:47
  447.9 0.0 slice-done.9
  447.9 14.2 %fusion.31 = f32[2048,2048]{1,0:T(8,128)} fusion(bf16[1280,2048]{1,0:T(8,128)(2,1)S(1)} %bitcast.57, bf16[1280,2048]{1,0:T(8,128)(2,1)S(1)} %get-tuple-element.49), kind=kOutput, calls=%fused_computation.56 | convolution fusion | flops 10737418240 | bytes 27262976 | tf_op jit(solution)/shard_map/ng,nh->gh/dot_general | solution.py:50
  462.1 21.2 %fusion.201 = (f32[2048]{0:T(1024)}, bf16[1280,2048]{1,0:T(8,128)(2,1)}) fusion(f32[1280,2048]{1,0:T(8,128)} %get-tuple-element.41, f32[2048]{0:T(1024)S(1)} %copy-done.8, bf16[2048,2048]{1,0:T(8,128)(2,1)} %param.20, bf16[1280,2048]{1,0:T(8,128)(2,1)S(1)} %get-tuple-element.49), kind=kOutput, calls=%fused_computation.273 | convolution fusion | flops 10774116352 | bytes 29376512 | tf_op jit(solution)/shard_map/nh,gh->ng/dot_general | solution.py:51
  483.3 13.0 %convolution_bitcast_fusion = f32[1536,2048]{0,1:T(8,128)} fusion(bf16[1280,1536]{1,0:T(8,128)(2,1)S(1)} %bitcast.45, bf16[1280,2048]{1,0:T(8,128)(2,1)} %get-tuple-element.47), kind=kOutput, calls=%fused_computation.50 | convolution fusion | flops 8053063680 | bytes 21757952 | tf_op jit(solution)/shard_map/nf,nh->fh/dot_general | solution.py:53
  496.3 12.6 %copy.35 = f32[1536,2048]{1,0:T(8,128)} copy(f32[1536,2048]{0,1:T(8,128)} %convolution_bitcast_fusion) | data formatting | bytes 25165824
  508.9 65.2 %copy.40 = f32[384,65536]{1,0:T(8,128)} copy(f32[384,65536]{1,0:T(8,128)} %proto_grads.1) | data formatting | bytes 201326592
  (45 shorter events, 0.1 us)
Async XLA Ops:
  7.2 15.9 %copy-start = (bf16[2048,384]{1,0:T(8,128)(2,1)S(1)}, bf16[2048,384]{1,0:T(8,128)(2,1)}, u32[]{:S(2)}) copy-start(bf16[2048,384]{1,0:T(8,128)(2,1)} %param.22) | copy-start | bytes 4718596
  7.2 422.8 %all-reduce.2.cloned.1.call-start = ((), (), s32[]{:S(2)}) async-start(), calls=%async_computation | async-start | bytes 3932160 | tf_op jit(solution)/shard_map/psum | solution.py:452
  8.0 192.6 %copy-start.7 = (f32[2048]{0:T(1024)}, f32[2048]{0:T(1024)S(1)}, u32[]{:S(2)}) copy-start(f32[2048]{0:T(1024)S(1)} %convert_element_type.83) | copy-start | bytes 24580
  8.7 0.7 copy-start.9
  9.4 13.7 %copy-start.11 = (f32[384]{0:T(512)}, f32[384]{0:T(512)S(1)}, u32[]{:S(2)}) copy-start(f32[384]{0:T(512)S(1)} %convert_element_type.87) | copy-start | bytes 4612
  9.4 14.3 %copy-start.13 = (bf16[2048]{0:T(1024)(128)(2,1)S(1)}, bf16[2048]{0:T(1024)(128)(2,1)}, u32[]{:S(2)}) copy-start(bf16[2048]{0:T(1024)(128)(2,1)} %param.26) | copy-start | bytes 12292
  9.4 14.3 %copy-start.14 = (bf16[2048]{0:T(1024)(128)(2,1)S(1)}, bf16[2048]{0:T(1024)(128)(2,1)}, u32[]{:S(2)}) copy-start(bf16[2048]{0:T(1024)(128)(2,1)} %param.28) | copy-start | bytes 12292
  9.4 14.3 %copy-start.15 = (bf16[384]{0:T(512)(128)(2,1)S(1)}, bf16[384]{0:T(512)(128)(2,1)}, u32[]{:S(2)}) copy-start(bf16[384]{0:T(512)(128)(2,1)} %param.30) | copy-start | bytes 2308
  9.4 14.4 %copy-start.16 = (bf16[32,1536]{1,0:T(8,128)(2,1)S(1)}, bf16[32,1536]{1,0:T(8,128)(2,1)}, u32[]{:S(2)}) copy-start(bf16[32,1536]{1,0:T(8,128)(2,1)} %param.17) | copy-start | bytes 294916
  54.1 1.3 copy-start.3
  55.4 3.4 slice-start
  129.8 6.5 %copy-start.1 = (bf16[10,128,384]{2,1,0:T(8,128)(2,1)S(1)}, bf16[10,128,384]{2,1,0:T(8,128)(2,1)}, u32[]{:S(2)}) copy-start(bf16[10,128,384]{2,1,0:T(8,128)(2,1)} %copy.30) | copy-start | bytes 2949124
  129.8 7.9 %copy-start.6 = (bf16[160,1536]{1,0:T(8,128)(2,1)S(1)}, bf16[160,1536]{1,0:T(8,128)(2,1)}, u32[]{:S(2)}) copy-start(bf16[160,1536]{1,0:T(8,128)(2,1)} %param.16) | copy-start | bytes 1474564
  137.8 62.9 %slice-start.3 = ((s8[6291456]{0:T(1024)(128)(4,1)}), s8[4194304]{0:T(1024)(128)(4,1)S(1)}, s32[]{:S(2)}) async-start(s8[6291456]{0:T(1024)(128)(4,1)} %bitcast.52), calls=%async_computation.4 | async-start | bytes 8388608
  196.7 4.0 slice-start.4
  196.7 36.7 %slice-start.1 = ((s8[8388608]{0:T(1024)(128)(4,1)}), s8[4194304]{0:T(1024)(128)(4,1)S(1)}, s32[]{:S(2)}) async-start(s8[8388608]{0:T(1024)(128)(4,1)} %bitcast.50), calls=%async_computation.2 | async-start | bytes 8388608
  200.6 32.8 %copy-start.4 = (bf16[8,160,1536]{2,1,0:T(8,128)(2,1)}, bf16[8,160,1536]{2,1,0:T(8,128)(2,1)S(1)}, u32[]{:S(2)}) copy-start(bf16[8,160,1536]{2,1,0:T(8,128)(2,1)S(1)} %convert_element_type.100) | copy-start | bytes 11796484
  200.7 32.7 %copy-start.10 = (f32[2048]{0:T(1024)S(1)}, f32[2048]{0:T(1024)}, u32[]{:S(2)}) copy-start(f32[2048]{0:T(1024)} %copy-done.9) | copy-start | bytes 24580
  200.7 32.7 %slice-start.2 = ((s8[8388608]{0:T(1024)(128)(4,1)}), s8[4194304]{0:T(1024)(128)(4,1)S(1)}, s32[]{:S(2)}) async-start(s8[8388608]{0:T(1024)(128)(4,1)} %bitcast.50), calls=%async_computation.3 | async-start | bytes 8388608
  233.4 36.0 %copy-start.17 = (bf16[1280,2048]{1,0:T(8,128)(2,1)}, bf16[1280,2048]{1,0:T(8,128)(2,1)S(1)}, u32[]{:S(2)}) copy-start(bf16[1280,2048]{1,0:T(8,128)(2,1)S(1)} %get-tuple-element.40) | copy-start | bytes 15728644
  269.4 123.2 %copy-start.12 = (f32[384]{0:T(512)S(1)}, f32[384]{0:T(512)}, u32[]{:S(2)}) copy-start(f32[384]{0:T(512)} %copy-done.11) | copy-start | bytes 4612
  430.0 2.1 copy-start.2
  430.0 10.7 %slice-start.5 = ((s8[10485760]{0:T(1024)(128)(4,1)}), s8[4194304]{0:T(1024)(128)(4,1)S(1)}, s32[]{:S(2)}) async-start(s8[10485760]{0:T(1024)(128)(4,1)} %bitcast.54), calls=%async_computation.6 | async-start | bytes 8388608
  432.1 8.6 %slice-start.6 = ((s8[10485760]{0:T(1024)(128)(4,1)}), s8[4194304]{0:T(1024)(128)(4,1)S(1)}, s32[]{:S(2)}) async-start(s8[10485760]{0:T(1024)(128)(4,1)} %bitcast.54), calls=%async_computation.7 | async-start | bytes 8388608
  433.2 7.5 %slice-start.7 = ((s8[10485760]{0:T(1024)(128)(4,1)}), s8[2097152]{0:T(1024)(128)(4,1)S(1)}, s32[]{:S(2)}) async-start(s8[10485760]{0:T(1024)(128)(4,1)} %bitcast.54), calls=%async_computation.8 | async-start | bytes 4194304
  433.2 14.7 %slice-start.8 = ((s8[5242880]{0:T(1024)(128)(4,1)}), s8[4194304]{0:T(1024)(128)(4,1)S(1)}, s32[]{:S(2)}) async-start(s8[5242880]{0:T(1024)(128)(4,1)} %bitcast.56), calls=%async_computation.9 | async-start | bytes 8388608
  440.7 7.2 %slice-start.9 = ((s8[5242880]{0:T(1024)(128)(4,1)}), s8[1048576]{0:T(1024)(128)(4,1)S(1)}, s32[]{:S(2)}) async-start(s8[5242880]{0:T(1024)(128)(4,1)} %bitcast.56), calls=%async_computation.10 | async-start | bytes 2097152
  447.9 14.2 %copy-start.8 = (f32[2048]{0:T(1024)S(1)}, f32[2048]{0:T(1024)}, u32[]{:S(2)}) copy-start(f32[2048]{0:T(1024)} %copy-done.7) | copy-start | bytes 24580
  462.0 21.2 %copy-start.5 = (bf16[8,160,1536]{2,1,0:T(8,128)(2,1)S(1)}, bf16[8,160,1536]{2,1,0:T(8,128)(2,1)}, u32[]{:S(2)}) copy-start(bf16[8,160,1536]{2,1,0:T(8,128)(2,1)} %copy-done.4) | copy-start | bytes 11796484
Sparse Core Ops, SparseCore 0:
  136.4 99.6 all-reduce.1
